TPU v7x, 512 devices: a 4x2x32 block of a 4x8x32 slice. The times are simulated.
512 devices in a mesh: grp: 2 (over y), seq: 32 (over z), head: 4 (over x), rep: 2 (over core).
Axes of the slice: x: 4, y: 2, z: 32, core: 2. Of those that a mesh axis runs over, the one named last changes fastest.
The devices are a block of a 4x8x32 slice.
Arguments:
- x_proj: bfloat16 [4, 32, 32, 4, 8192], P(('grp', 'rep'), None, 'seq', None, 'head'), parts along dimension 0, may hold values from -6 to 6
- gate_proj: bfloat16 [4, 32, 32, 4, 8192], P(('grp', 'rep'), None, 'seq', None, 'head'), parts along dimension 0, may hold values from -6 to 6
- bc_proj: bfloat16 [4, 32, 32, 4, 256], P(('grp', 'rep'), None, 'seq'), parts along dimension 0, may hold values from -6 to 6
- dt_proj: bfloat16 [4, 32, 32, 4, 128], P(('grp', 'rep'), None, 'seq', None, 'head'), parts along dimension 0, may hold values from -5.5 to 7.5
- a_rate: float32 [128], P('head'), may hold values from 2.4414063e-05 to 0.05
- dt_bias: float32 [128], P('head'), may hold values from -1 to 1
- d_skip: float32 [128], P('head'), may hold values from 0.5 to 1.5
- conv_x_weight: float32 [4, 8192], P(None, 'head'), may hold values from -3 to 3
- conv_bc_weight: float32 [4, 256], replicated, may hold values from -3 to 3
- norm_gain: float32 [8192], P('head'), may hold values from 0.1 to 1.9
- out_weight: bfloat16 [8192, 2048], P(('seq', 'rep'), 'head'), may hold values from -0.0625 to 0.0625
- request_first_position: int32 [4], P(('grp', 'rep')), parts along dimension 0, may hold values from 0 to 2047
- owner: int32 [4, 32], P(('grp', 'rep')), parts along dimension 0, may hold values from 0 to 31, each once within a row
Outputs:
- mixed: bfloat16 [4, 4096, 2048], P(('grp', 'rep'), 'seq', 'head'), parts along dimension 0
- ssm_state: float32 [4, 32, 128, 256], P(('grp', 'rep'), 'seq', 'head'), parts along dimension 0
- conv_x_state: bfloat16 [4, 32, 3, 256], P(('grp', 'rep'), 'seq', None, 'head'), parts along dimension 0
- conv_bc_state: bfloat16 [4, 32, 3, 8], P(('grp', 'rep'), 'seq'), parts along dimension 0
There are 2 independent parts, one for each index of `grp`. A program takes and returns all parts, laid end to end along the dimension named above; an argument that names none is the same for every part. Nothing has to cross between parts.
Inputs may be any that keep to these rules, and one draw needn't show every extreme that they name: Each row of owner names every index of seq once.
All inputs are finite; a program needn't handle non-finite values.
Results may differ from a plain program's by a relative error of at most 0.007.
Values may be sent and summed in bfloat16 or wider, within the bound.
A program may use at most 128 MiB of HBM per device.

v0:
```python
import jax
import jax.numpy as jnp
from jax import lax
from jax.sharding import PartitionSpec as P

HEAD_DIM = 64
NSTATE = 128
KCONV = 4
SPAN = 128
INNER = 8192
highest = lax.Precision.HIGHEST
stability_constant = 1e-05


def side_by_side(arrays, axis, split_dim, concat_dim, along):
    ends, at = ([], 0)
    for a in arrays[:-1]:
        at += a.shape[along]
        ends.append(at)
    both = jnp.concatenate(arrays, axis=along)
    return tuple(
        jnp.split(
            lax.all_to_all(both, axis, split_axis=split_dim, concat_axis=concat_dim, tiled=True),
            ends,
            axis=along,
        )
    )


def passed_along(value, axis, by):
    devices = lax.axis_size(axis)
    pairs = [(i, i + by) for i in range(devices) if 0 <= i + by < devices]
    return lax.ppermute(value, axis, pairs)


def prefix(value, axis, combine, identity):
    devices, place = (lax.axis_size(axis), lax.axis_index(axis))
    everything = jax.tree.map(lambda part: lax.all_gather(part, axis), value)
    start = jax.tree.map(
        lambda part, zero: jnp.broadcast_to(jnp.asarray(zero, part.dtype), part.shape),
        value,
        identity,
    )

    def lap(k, before):
        reached = k < place
        new = combine(before, jax.tree.map(lambda part: part[k], everything))
        return jax.tree.map(lambda a, b: jnp.where(reached, a, b), new, before)

    return lax.fori_loop(0, devices, lap, start)


def broadcast(block, axis, source):
    block = jnp.where(lax.axis_index(axis) == source, block, jnp.zeros_like(block))
    return lax.psum(block, axis)


def span_terms(x_conv, b_rows, c_rows, step_size, log_decay):
    cum_decay = jnp.cumsum(log_decay, axis=1)
    scores = jnp.einsum("kqn,ktn->kqt", c_rows, b_rows, preferred_element_type=jnp.float32)
    cum_heads = jnp.swapaxes(cum_decay, 1, 2)
    step_heads = jnp.swapaxes(step_size, 1, 2)
    block_len = cum_decay.shape[1]
    causal = jnp.arange(block_len)[:, None] >= jnp.arange(block_len)[None, :]
    decay_gap = cum_heads[:, :, :, None] - cum_heads[:, :, None, :]
    seg_decay = jnp.exp(jnp.where(causal, decay_gap, -jnp.inf))
    weights = (scores[:, None] * seg_decay * step_heads[:, :, None, :]).astype(jnp.bfloat16)
    y_intra = jnp.einsum("khqt,kthp->kqhp", weights, x_conv, preferred_element_type=jnp.float32)
    remaining_length = jnp.exp(cum_decay[:, -1:, :] - cum_decay)
    scaled = ((remaining_length * step_size)[..., None] * x_conv.astype(jnp.float32)).astype(
        jnp.bfloat16
    )
    states = jnp.einsum("kthp,ktn->khpn", scaled, b_rows, preferred_element_type=jnp.float32)
    return (cum_decay, y_intra, states, jnp.exp(cum_decay[:, -1, :]))


def conv_silu(preceding_tokens, current, weight):
    extended = jnp.concatenate([preceding_tokens, current], axis=0)
    length = current.shape[0]
    accum = jnp.zeros(current.shape, jnp.float32)
    for offset in range(weight.shape[0]):
        accum = accum + weight[offset] * extended[offset : offset + length].astype(jnp.float32)
    return jax.nn.silu(accum)


def link(preceding_tokens, later):
    return (
        preceding_tokens[0] * later[0],
        later[0][:, None, None] * preceding_tokens[1] + later[1],
    )


def add_rows(source, piece):
    return jnp.dot(source, piece, preferred_element_type=jnp.float32)


def take_slab(values, slab_index, seq_count):
    grouped = values.reshape(values.shape[0], seq_count, -1)
    return lax.dynamic_index_in_dim(grouped, slab_index, axis=1, keepdims=False)


def local(
    x_proj,
    gate_proj,
    bc_proj,
    dt_proj,
    a_rate,
    dt_bias,
    d_skip,
    conv_x_weight,
    conv_bc_weight,
    norm_gain,
    out_weight,
    request_first_position,
    owner,
):
    x_all, z_all, bc_all, dt_all = side_by_side(
        (x_proj, gate_proj, bc_proj, dt_proj), "seq", 1, 2, 4
    )
    tokens_here = x_all.shape[2] * x_all.shape[3]
    x_local = x_all.reshape(tokens_here, x_all.shape[4])
    z_local = z_all.reshape(tokens_here, z_all.shape[4])
    bc_local = bc_all.reshape(tokens_here, bc_all.shape[4])
    dt_local = dt_all.reshape(tokens_here, dt_all.shape[4])
    heads = dt_local.shape[1]
    seq_index = lax.axis_index("seq")
    seq_count = lax.axis_size("seq")
    positions = seq_index * tokens_here + jnp.arange(tokens_here, dtype=jnp.int32)
    is_live = positions >= request_first_position[0]
    x_live = jnp.where(is_live[:, None], x_local, jnp.zeros_like(x_local))
    bc_live = jnp.where(is_live[:, None], bc_local, jnp.zeros_like(bc_local))
    rim_rows = KCONV - 1
    tail_x = x_live[tokens_here - rim_rows :]
    tail_bc = bc_live[tokens_here - rim_rows :]
    before_x, before_bc = passed_along((tail_x, tail_bc), "seq", 1)
    x_conv = conv_silu(before_x, x_live, conv_x_weight).astype(jnp.bfloat16)
    bc_conv = conv_silu(before_bc, bc_live, conv_bc_weight).astype(jnp.bfloat16)
    step_size = (
        jax.nn.softplus(dt_local.astype(jnp.float32) + dt_bias)
        * is_live.astype(jnp.float32)[:, None]
    )
    log_decay = -a_rate * step_size
    blocks = tokens_here // SPAN
    x_blocks = x_conv.reshape(blocks, SPAN, heads, HEAD_DIM)
    b_blocks = bc_conv[:, :NSTATE].reshape(blocks, SPAN, NSTATE)
    c_blocks = bc_conv[:, NSTATE:].reshape(blocks, SPAN, NSTATE)
    cum_decay, y_intra, states, decays = span_terms(
        x_blocks,
        b_blocks,
        c_blocks,
        step_size.reshape(blocks, SPAN, heads),
        log_decay.reshape(blocks, SPAN, heads),
    )

    def advance(carry, inputs):
        factor, contrib = inputs
        return (factor[:, None, None] * carry + contrib, carry)

    zero_state = jnp.zeros((heads, HEAD_DIM, NSTATE), jnp.float32)
    local_final, local_enter = lax.scan(advance, zero_state, (decays, states))
    dev_decay = jnp.prod(decays, axis=0)
    ones_heads = jnp.ones((heads,), jnp.float32)
    enter_decay, enter_state = prefix(
        (dev_decay, local_final), "seq", link, (ones_heads, zero_state)
    )
    c_wide = c_blocks.astype(jnp.float32)
    before_block = jnp.concatenate([ones_heads[None], jnp.cumprod(decays, axis=0)[:-1]], axis=0)
    entering = local_enter + before_block[:, :, None, None] * enter_state[None]
    y_state = jnp.exp(cum_decay)[..., None] * jnp.einsum(
        "kqn,khpn->kqhp", c_wide, entering, precision=highest
    )
    y_total = y_intra + y_state + d_skip[:, None] * x_blocks.astype(jnp.float32)
    y_flat = y_total.reshape(tokens_here, heads * HEAD_DIM)
    gated = y_flat * jax.nn.silu(z_local.astype(jnp.float32))
    square_sums = lax.psum(jnp.sum(gated * gated, axis=1), "head")
    normed = (
        gated * lax.rsqrt(square_sums[:, None] / INNER + stability_constant) * norm_gain
    ).astype(jnp.bfloat16)
    last_index = seq_count - 1
    own_final = dev_decay[:, None, None] * enter_state + local_final
    final_state, keep_x, keep_bc = (
        broadcast(own_final, "seq", last_index),
        broadcast(tail_x.astype(jnp.float32), "seq", last_index).astype(tail_x.dtype),
        broadcast(tail_bc.astype(jnp.float32), "seq", last_index).astype(tail_bc.dtype),
    )
    slab_index = jnp.sum(
        jnp.where(owner[0] == seq_index, jnp.arange(seq_count, dtype=jnp.int32), 0)
    )
    ssm_state = take_slab(final_state.reshape(heads, -1), slab_index, seq_count)[None, None]
    conv_x_state = take_slab(keep_x, slab_index, seq_count)[None, None]
    conv_bc_state = take_slab(keep_bc, slab_index, seq_count)[None, None]
    features = lax.all_gather(normed, "head", axis=1, tiled=True)
    out_cols = out_weight.shape[1]
    mixed_sum = add_rows(features, lax.all_gather(out_weight, ("seq", "rep"), axis=0, tiled=True))
    mixed = mixed_sum.astype(jnp.bfloat16).reshape(1, tokens_here, out_cols)
    return (mixed, ssm_state, conv_x_state, conv_bc_state)


def solution(mesh):
    return jax.shard_map(
        local,
        mesh=mesh,
        in_specs=(
            P(("grp", "rep"), None, "seq", None, "head"),
            P(("grp", "rep"), None, "seq", None, "head"),
            P(("grp", "rep"), None, "seq", None, None),
            P(("grp", "rep"), None, "seq", None, "head"),
            P("head"),
            P("head"),
            P("head"),
            P(None, "head"),
            P(),
            P("head"),
            P(("seq", "rep"), "head"),
            P(("grp", "rep")),
            P(("grp", "rep"), None),
        ),
        out_specs=(
            P(("grp", "rep"), "seq", "head"),
            P(("grp", "rep"), "seq", "head", None),
            P(("grp", "rep"), "seq", None, "head"),
            P(("grp", "rep"), "seq", None, None),
        ),
        check_vma=False,
    )
```

profile of v0, /device:TPU:34, one launch (start us, length us, event | category | flops | bytes accessed | tf_op | source)
XLA Modules:
  0.0 893.1 jit_solution(16891518025906551019)
XLA Ops:
  8.1 2.9 pad_maximum_fusion
  10.9 45.8 %all-to-all-start = ((bf16[1,32,1,4,4384]{4,3,2,0,1:T(4,128)(2,1)}), bf16[1,32,1,4,4384]{4,3,2,0,1:T(4,128)(2,1)S(1)}, u32[]{:S(2)}, u32[]{:S(2)}) async-start(bf16[1,32,1,4,4384]{4,3,2,0,1:T(4,128)(2,1)} %pad_maximum_fusion), calls=%async_computation | async-start | bytes 2293760 | tf_op jit(solution)/shard_map/all_to_all | solution.py:23
  57.5 111.5 %all-to-all-done = bf16[1,32,1,4,4384]{4,3,2,0,1:T(4,128)(2,1)S(1)} async-done(((bf16[1,32,1,4,4384]{4,3,2,0,1:T(4,128)(2,1)}), bf16[1,32,1,4,4384]{4,3,2,0,1:T(4,128)(2,1)S(1)}, u32[]{:S(2)}, u32[]{:S(2)}) %all-to-all-start) | async-done | bytes 1122336 | tf_op jit(solution)/shard_map/all_to_all | solution.py:23
  170.6 3.9 collective-permute-start
  174.6 1.9 collective-permute-start.1
  176.7 8.4 collective-permute-done.1
  185.2 2.9 fusion.8
  189.6 58.3 %all-gather = f32[32,1,32]{2,1,0:T(1,128)S(1)} all-gather(f32[1,1,32]{2,1,0:T(1,128)S(1)} %get-tuple-element.155), channel_id=2, replica_groups=mesh['grp'=2,'seq'=32,'head'=4,'rep'=2] {'seq'}, dimensions={0}, use_global_device_ids=true | all-gather | bytes 4224 | tf_op jit(solution)/shard_map/all_gather | solution.py:38
  247.8 311.1 %all-gather.10.cloned.1.call-done = f32[1024,64,128]{2,1,0:T(8,128)} async-done(((f32[32,64,128]{2,1,0:T(8,128)}), f32[1024,64,128]{2,1,0:T(8,128)}) %all-gather.10.cloned.1.call-update) | async-done | bytes 33554448 | tf_op jit(solution)/shard_map/all_gather | solution.py:38
  559.0 48.1 %while.9 = (s32[]{:T(128)}, f32[32,64,128]{2,1,0:T(8,128)S(1)}, s32[]{:T(128)}, f32[32,32]{1,0:T(8,128)S(1)}, f32[32,32,64,128]{3,2,1,0:T(8,128)}, /*index=5*/s32[]{:T(128)}, s32[]{:T(128)}) while((s32[]{:T(128)}, f32[32,64,128]{2,1,0:T(8,128)S(1)}, s32[]{:T(128)}, f32[32,32]{1,0:T(8,128)S(1)}, f32[32,32,64,128]{3,2,1,0:T(8,128)}, ...), condition=%wide.region_2.3_spmd.clone, body=%wide.region_1.2_spmd.clone.sunk | while | flops 1048580 | bytes 3146217 | solution.py:50
  559.0 1.5 fusion.43
  560.5 1.5 fusion.43
  562.0 1.5 fusion.43
  563.6 1.5 fusion.43
  565.1 1.5 fusion.43
  566.6 1.5 fusion.43
  568.1 1.5 fusion.43
  569.6 1.5 fusion.43
  571.1 1.5 fusion.43
  572.6 1.5 fusion.43
  574.1 1.5 fusion.43
  575.6 1.5 fusion.43
  577.1 1.5 fusion.43
  578.6 1.5 fusion.43
  580.1 1.5 fusion.43
  581.6 1.5 fusion.43
  583.1 1.5 fusion.43
  584.6 1.5 fusion.43
  586.1 1.5 fusion.43
  587.6 1.5 fusion.43
  589.1 1.5 fusion.43
  590.6 1.5 fusion.43
  592.1 1.5 fusion.43
  593.6 1.5 fusion.43
  595.1 1.5 fusion.43
  596.6 1.5 fusion.43
  598.1 1.5 fusion.43
  599.6 1.5 fusion.43
  601.1 1.5 fusion.43
  602.6 1.5 fusion.43
  605.6 1.5 fusion.43
  608.3 2.5 reshape_reshape.3
  611.6 2.4 reshape.434
  615.5 3.8 copy.93
  622.1 8.8 psum.28
  635.0 137.0 %all-reduce = (bf16[3,2048]{0,1:T(8,128)(2,1)S(1)}, bf16[3,256]{1,0:T(4,128)(2,1)S(1)}) all-reduce(f32[3,2048]{0,1:T(8,128)S(1)} %convert_select_fusion, f32[3,256]{1,0:T(4,128)S(1)} %convert_select_fusion.1), channel_id=1, replica_groups=mesh['grp'=2,'seq'=32,'head'=4,'rep'=2] {'seq'}, use_global_device_ids=true, to_apply=%region_7.8 | all-reduce | flops 6912 | bytes 41472 | tf_op jit(solution)/shard_map/psum | solution.py:55
  773.3 104.8 %all-reduce.3.cloned.1.call-done = f32[32,32,256]{2,1,0:T(8,128)} async-done(((f32[32,32,256]{2,1,0:T(8,128)}), f32[32,32,256]{2,1,0:T(8,128)}) %all-reduce.3.cloned.1.call-update) | async-done | bytes 1048592 | tf_op jit(solution)/shard_map/psum | solution.py:55
  879.7 6.0 fusion.4
  (115 shorter events, 16.3 us)
Async XLA Ops:
  8.0 49.4 %copy-start.10 = (f32[32]{0:T(128)S(1)}, f32[32]{0:T(128)}, u32[]{:S(2)}) copy-start(f32[32]{0:T(128)} %param.19) | copy-start | bytes 388
  8.0 49.4 %copy-start.8 = (f32[4,256]{1,0:T(4,128)S(1)}, f32[4,256]{1,0:T(4,128)}, u32[]{:S(2)}) copy-start(f32[4,256]{1,0:T(4,128)} %param.23) | copy-start | bytes 12292
  8.1 49.4 %copy-start.6 = (f32[4,2048]{1,0:T(4,128)S(1)}, f32[4,2048]{1,0:T(4,128)}, u32[]{:S(2)}) copy-start(f32[4,2048]{1,0:T(4,128)} %param.22) | copy-start | bytes 98308
  8.1 161.0 %copy-start.9 = (f32[32]{0:T(128)S(1)}, f32[32]{0:T(128)}, u32[]{:S(2)}) copy-start(f32[32]{0:T(128)} %param.20) | copy-start | bytes 388
  10.9 158.1 %all-to-all-start = ((bf16[1,32,1,4,4384]{4,3,2,0,1:T(4,128)(2,1)}), bf16[1,32,1,4,4384]{4,3,2,0,1:T(4,128)(2,1)S(1)}, u32[]{:S(2)}, u32[]{:S(2)}) async-start(bf16[1,32,1,4,4384]{4,3,2,0,1:T(4,128)(2,1)} %pad_maximum_fusion), calls=%async_computation | async-start | bytes 2293760 | tf_op jit(solution)/shard_map/all_to_all | solution.py:23
  56.7 502.2 %all-gather.10.cloned.1.call-start = ((), (), s32[]{:S(2)}) async-start(), calls=%async_computation.4 | async-start | bytes 34603008 | tf_op jit(solution)/shard_map/all_gather | solution.py:38
  170.3 19.1 %copy-start.1 = (bf16[128,2048]{0,1:T(8,128)(2,1)}, bf16[128,2048]{0,1:T(8,128)(2,1)S(1)}, u32[]{:S(2)}) copy-start(bf16[128,2048]{0,1:T(8,128)(2,1)S(1)} %broadcast_select_fusion) | copy-start | bytes 1572868
  170.6 14.6 %collective-permute-start = (bf16[3,2048]{0,1:T(8,128)(2,1)S(1)}, bf16[3,2048]{0,1:T(8,128)(2,1)S(1)}, u32[]{:S(2)}, u32[]{:S(2)}) collective-permute-start(bf16[3,2048]{0,1:T(8,128)(2,1)S(1)} %slice.77), channel_id=1, source_target_pairs={{0,8},{8,16},{16,24},{24,32},{32,40},{40,48},{48,56},{56,64},{64,7... | collective-permute-start | bytes 36872 | tf_op jit(solution)/shard_map/ppermute | solution.py:33
  174.6 10.5 %collective-permute-start.1 = (bf16[3,256]{1,0:T(4,128)(2,1)S(1)}, bf16[3,256]{1,0:T(4,128)(2,1)S(1)}, u32[]{:S(2)}, u32[]{:S(2)}) collective-permute-start(bf16[3,256]{1,0:T(4,128)(2,1)S(1)} %slice.82), channel_id=1, source_target_pairs={{0,8},{8,16},{16,24},{24,32},{32,40},{40,48},{48,56},{56,64},{64,7... | collective-permute-start | bytes 4616 | tf_op jit(solution)/shard_map/ppermute | solution.py:33
  189.5 688.6 %all-reduce.3.cloned.1.call-start = ((), (), s32[]{:S(2)}) async-start(), calls=%async_computation.3 | async-start | bytes 2097152 | tf_op jit(solution)/shard_map/psum | solution.py:55
  559.0 48.1 %copy-start = (f32[32,64,128]{2,1,0:T(8,128)S(1)}, f32[32,64,128]{2,1,0:T(8,128)}, u32[]{:S(2)}) copy-start(f32[32,64,128]{2,1,0:T(8,128)} %convolution_add_fusion) | copy-start | bytes 3145732
  610.8 268.8 %all-gather.8.cloned.1.call-start = ((), (), s32[]{:S(2)}) async-start(), calls=%async_computation.2 | async-start | bytes 8519680 | tf_op jit(solution)/shard_map/all_gather | solution.py:194
  611.5 268.2 %all-gather.6.cloned.1.call-start = ((), (), s32[]{:S(2)}) async-start(), calls=%async_computation.1 | async-start | bytes 2621440 | tf_op jit(solution)/shard_map/all_gather | solution.py:192
  615.3 3.9 copy-start.3
  619.3 1.1 copy-start.11
  619.6 1.2 copy-start.4
  619.6 1.4 copy-start.5
  621.0 9.9 %copy-start.7 = (f32[2048]{0:T(1024)S(1)}, f32[2048]{0:T(1024)}, u32[]{:S(2)}) copy-start(f32[2048]{0:T(1024)} %param.24) | copy-start | bytes 24580
  622.1 10.1 %copy-start.12 = (s32[1,32]{1,0:T(1,128)S(1)}, s32[1,32]{1,0:T(1,128)}, u32[]{:S(2)}) copy-start(s32[1,32]{1,0:T(1,128)} %param.27) | copy-start | bytes 388
  622.1 12.7 %copy-start.2 = (bf16[128,2048]{0,1:T(8,128)(2,1)S(1)}, bf16[128,2048]{0,1:T(8,128)(2,1)}, u32[]{:S(2)}) copy-start(bf16[128,2048]{0,1:T(8,128)(2,1)} %copy-done.1) | copy-start | bytes 1572868
Sparse Core Ops, SparseCore 0:
  189.6 369.2 all-gather.9
  611.0 267.0 all-reduce.2
Sparse Core Ops, SparseCore 1:
  613.5 145.7 all-gather.7
  761.3 36.1 all-gather.5
where the time goes:
time: 895 us; the launch traced here: 893 us
  waiting for transfers between devices  537 us (60%)
  blocking collectives  204 us (23%)
  other arithmetic  56.9 us (6%)
  starting transfers between devices  51.9 us (6%)
  between operations  18.5 us (2%)
  local copies, waits for them, and re-layouts  15.2 us (2%)
  matrix products  9.14 us (1%)
    all_gather x1, waiting for transfers between devices, prefix(): everything = jax.tree.map(lambda part: lax.all_gather(part, axis), value)  311 us
    psum x1, blocking collectives, broadcast(): return lax.psum(block, axis)  137 us
    all_to_all x1, waiting for transfers between devices, side_by_side(): lax.all_to_all(both, axis, split_axis=split_dim, concat_axis=concat_dim,...  112 us
    psum x1, waiting for transfers between devices, broadcast(): return lax.psum(block, axis)  105 us
    all_gather x1, blocking collectives, prefix(): everything = jax.tree.map(lambda part: lax.all_gather(part, axis), value)  58.3 us
    select_n x32, other arithmetic, lap(): return jax.tree.map(lambda a, b: jnp.where(reached, a, b), new, before)  46.9 us
    all_to_all x1, starting transfers between devices, side_by_side(): lax.all_to_all(both, axis, split_axis=split_dim, concat_axis=concat_dim,...  45.8 us
  transfers between devices with their start and end apart: 7, of which 4 were waited for; matrix products, arithmetic and copies ran while one was open for 2% of the time, Pallas kernels for 0%

commit v1 on v0

--- a/solution.py
+++ b/solution.py
@@ -52,7 +52,7 @@
 
 def broadcast(block, axis, source):
     block = jnp.where(lax.axis_index(axis) == source, block, jnp.zeros_like(block))
-    return lax.psum(block, axis)
+    return jnp.sum(lax.all_gather(block, axis), axis=0)
 
 
 def span_terms(x_conv, b_rows, c_rows, step_size, log_decay):

time: 895 us -> 1140 us (1.27)
  the two profiles are of different devices: /device:TPU:34 before, /device:TPU:33 now
where the time goes in v1:
time: 1140 us
  waiting for transfers between devices  818 us (72%)
  blocking collectives  155 us (14%)
  other arithmetic  69.8 us (6%)
  starting transfers between devices  51.6 us (5%)
  between operations  16.8 us (1%)
  local copies, waits for them, and re-layouts  15.9 us (1%)
    all_gather x1, waiting for transfers between devices, broadcast(): return jnp.sum(lax.all_gather(block, axis), axis=0)  377 us
    all_gather x1, waiting for transfers between devices, prefix(): everything = jax.tree.map(lambda part: lax.all_gather(part, axis), value)  315 us
    all_to_all x1, waiting for transfers between devices, side_by_side(): lax.all_to_all(both, axis, split_axis=split_dim, concat_axis=concat_dim,...  112 us
    all_gather x2, blocking collectives, broadcast(): return jnp.sum(lax.all_gather(block, axis), axis=0)  97.9 us
    all_gather x1, blocking collectives, prefix(): everything = jax.tree.map(lambda part: lax.all_gather(part, axis), value)  48.6 us
    select_n x32, other arithmetic, lap(): return jax.tree.map(lambda a, b: jnp.where(reached, a, b), new, before)  46.9 us
    all_to_all x1, starting transfers between devices, side_by_side(): lax.all_to_all(both, axis, split_axis=split_dim, concat_axis=concat_dim,...  46.3 us
  transfers between devices with their start and end apart: 7, of which 5 were waited for; matrix products, arithmetic and copies ran while one was open for 7% of the time, Pallas kernels for 0%

profile of v1, /device:TPU:33, one launch (start us, length us, event | category | flops | bytes accessed | tf_op | source)
XLA Modules:
  0.0 1138.2 jit_solution(5737713382696392021)
XLA Ops:
  7.2 2.9 pad_maximum_fusion
  10.1 46.3 %all-to-all-start = ((bf16[1,32,1,4,4384]{4,3,2,0,1:T(4,128)(2,1)}), bf16[1,32,1,4,4384]{4,3,2,0,1:T(4,128)(2,1)S(1)}, u32[]{:S(2)}, u32[]{:S(2)}) async-start(bf16[1,32,1,4,4384]{4,3,2,0,1:T(4,128)(2,1)} %pad_maximum_fusion), calls=%async_computation | async-start | bytes 2293760 | tf_op jit(solution)/shard_map/all_to_all | solution.py:23
  57.2 111.7 %all-to-all-done = bf16[1,32,1,4,4384]{4,3,2,0,1:T(4,128)(2,1)S(1)} async-done(((bf16[1,32,1,4,4384]{4,3,2,0,1:T(4,128)(2,1)}), bf16[1,32,1,4,4384]{4,3,2,0,1:T(4,128)(2,1)S(1)}, u32[]{:S(2)}, u32[]{:S(2)}) %all-to-all-start) | async-done | bytes 1122336 | tf_op jit(solution)/shard_map/all_to_all | solution.py:23
  170.1 3.1 collective-permute-start.1
  174.7 2.0 collective-permute-start
  177.5 2.0 multiply_convert_fusion.3
  181.9 2.4 reshape.432
  185.8 2.7 copy.129
  188.5 48.6 %all-gather = f32[32,1,32]{2,1,0:T(1,128)S(1)} all-gather(f32[1,1,32]{2,1,0:T(1,128)S(1)} %get-tuple-element.153), channel_id=2, replica_groups=mesh['grp'=2,'seq'=32,'head'=4,'rep'=2] {'seq'}, dimensions={0}, use_global_device_ids=true | all-gather | bytes 4224 | tf_op jit(solution)/shard_map/all_gather | solution.py:38
  238.6 314.9 %all-gather.16.cloned.1.call-done = f32[1024,64,128]{2,1,0:T(8,128)} async-done(((f32[32,64,128]{2,1,0:T(8,128)}), f32[1024,64,128]{2,1,0:T(8,128)}) %all-gather.16.cloned.1.call-update) | async-done | bytes 33554448 | tf_op jit(solution)/shard_map/all_gather | solution.py:38
  553.5 48.2 %while.9 = (s32[]{:T(128)}, f32[32,64,128]{2,1,0:T(8,128)S(1)}, s32[]{:T(128)}, f32[32,32]{1,0:T(8,128)S(1)}, f32[32,32,64,128]{3,2,1,0:T(8,128)}, /*index=5*/s32[]{:T(128)}, s32[]{:T(128)}) while((s32[]{:T(128)}, f32[32,64,128]{2,1,0:T(8,128)S(1)}, s32[]{:T(128)}, f32[32,32]{1,0:T(8,128)S(1)}, f32[32,32,64,128]{3,2,1,0:T(8,128)}, ...), condition=%wide.region_2.3_spmd.clone, body=%wide.region_1.2_spmd.clone.sunk | while | flops 1048580 | bytes 3146217 | solution.py:50
  555.0 1.5 fusion.39
  556.5 1.5 fusion.39
  558.0 1.5 fusion.39
  559.5 1.5 fusion.39
  561.0 1.5 fusion.39
  562.5 1.5 fusion.39
  564.0 1.5 fusion.39
  565.5 1.5 fusion.39
  567.0 1.5 fusion.39
  568.5 1.5 fusion.39
  570.0 1.5 fusion.39
  573.0 1.5 fusion.39
  574.5 1.5 fusion.39
  576.0 1.5 fusion.39
  577.5 1.5 fusion.39
  579.0 1.5 fusion.39
  580.5 1.5 fusion.39
  582.1 1.5 fusion.39
  583.6 1.5 fusion.39
  585.1 1.5 fusion.39
  586.6 1.5 fusion.39
  588.1 1.5 fusion.39
  589.6 1.5 fusion.39
  592.6 1.5 fusion.39
  594.2 1.5 fusion.39
  595.7 1.5 fusion.39
  600.2 1.5 fusion.39
  602.9 2.0 multiply_reduce_fusion
  605.0 2.6 copy.127
  607.6 8.6 psum.7
  616.2 2.4 multiply_convert_fusion.2
  623.3 55.6 %all-gather.5 = f32[32,3,2048]{2,1,0:T(4,128)S(1)} all-gather(f32[1,3,2048]{2,1,0:T(4,128)S(1)} %select_bitcast_fusion), channel_id=5, replica_groups=mesh['grp'=2,'seq'=32,'head'=4,'rep'=2] {'seq'}, dimensions={0}, use_global_device_ids=true | all-gather | bytes 811008 | tf_op jit(solution)/shard_map/all_gather | solution.py:55
  679.8 42.4 %all-gather.6 = f32[32,3,256]{2,1,0:T(4,128)S(1)} all-gather(f32[1,3,256]{2,1,0:T(4,128)S(1)} %select_bitcast_fusion.1), channel_id=6, replica_groups=mesh['grp'=2,'seq'=32,'head'=4,'rep'=2] {'seq'}, dimensions={0}, use_global_device_ids=true | all-gather | bytes 101376 | tf_op jit(solution)/shard_map/all_gather | solution.py:55
  722.9 13.4 %all-gather.12.cloned.1.call-done = bf16[128,8192]{1,0:T(8,128)(2,1)} async-done(((bf16[128,2048]{1,0:T(8,128)(2,1)}), bf16[128,8192]{1,0:T(8,128)(2,1)}) %all-gather.12.cloned.1.call-update) | async-done | bytes 2097168 | tf_op jit(solution)/shard_map/all_gather | solution.py:192
  736.3 5.9 fusion.4
  742.2 376.6 %all-gather.18.cloned.1.call-done = f32[1024,64,128]{2,1,0:T(8,128)} async-done(((f32[32,64,128]{2,1,0:T(8,128)}), f32[1024,64,128]{2,1,0:T(8,128)}) %all-gather.18.cloned.1.call-update) | async-done | bytes 33554448 | tf_op jit(solution)/shard_map/all_gather | solution.py:55
  1118.8 11.8 %reduce_sum.46 = f32[32,64,128]{2,1,0:T(8,128)S(1)} reduce(f32[32,32,64,128]{3,2,1,0:T(8,128)} %bitcast.95, f32[]{:T(128)} %constant.79.clone.1), dimensions={0}, to_apply=%region_5.6 | reduce | flops 8126464 | bytes 34603012 | tf_op jit(solution)/shard_map/reduce_sum | solution.py:55
  (120 shorter events, 23.1 us)
Async XLA Ops:
  7.2 49.9 %copy-start.8 = (f32[32]{0:T(128)S(1)}, f32[32]{0:T(128)}, u32[]{:S(2)}) copy-start(f32[32]{0:T(128)} %param.19) | copy-start | bytes 388
  7.2 50.0 %copy-start.6 = (f32[4,256]{1,0:T(4,128)S(1)}, f32[4,256]{1,0:T(4,128)}, u32[]{:S(2)}) copy-start(f32[4,256]{1,0:T(4,128)} %param.23) | copy-start | bytes 12292
  7.2 50.0 %copy-start.4 = (f32[4,2048]{1,0:T(4,128)S(1)}, f32[4,2048]{1,0:T(4,128)}, u32[]{:S(2)}) copy-start(f32[4,2048]{1,0:T(4,128)} %param.22) | copy-start | bytes 98308
  7.2 161.7 %copy-start.7 = (f32[32]{0:T(128)S(1)}, f32[32]{0:T(128)}, u32[]{:S(2)}) copy-start(f32[32]{0:T(128)} %param.20) | copy-start | bytes 388
  10.1 158.8 %all-to-all-start = ((bf16[1,32,1,4,4384]{4,3,2,0,1:T(4,128)(2,1)}), bf16[1,32,1,4,4384]{4,3,2,0,1:T(4,128)(2,1)S(1)}, u32[]{:S(2)}, u32[]{:S(2)}) async-start(bf16[1,32,1,4,4384]{4,3,2,0,1:T(4,128)(2,1)} %pad_maximum_fusion), calls=%async_computation | async-start | bytes 2293760 | tf_op jit(solution)/shard_map/all_to_all | solution.py:23
  56.4 497.1 %all-gather.16.cloned.1.call-start = ((), (), s32[]{:S(2)}) async-start(), calls=%async_computation.3 | async-start | bytes 34603008 | tf_op jit(solution)/shard_map/all_gather | solution.py:38
  170.0 9.5 copy-start.2
  170.1 6.6 collective-permute-start.1
  174.7 2.8 collective-permute-start
  181.0 541.8 %all-gather.14.cloned.1.call-start = ((), (), s32[]{:S(2)}) async-start(), calls=%async_computation.2 | async-start | bytes 8519680 | tf_op jit(solution)/shard_map/all_gather | solution.py:194
  181.8 554.4 %all-gather.12.cloned.1.call-start = ((), (), s32[]{:S(2)}) async-start(), calls=%async_computation.1 | async-start | bytes 2621440 | tf_op jit(solution)/shard_map/all_gather | solution.py:192
  601.7 1.2 copy-start.3
  601.7 1.2 copy-start.9
  605.0 11.2 copy-start.1
  605.0 11.2 copy-start.5
  607.6 11.1 copy-start
  618.7 500.1 %all-gather.18.cloned.1.call-start = ((), (), s32[]{:S(2)}) async-start(), calls=%async_computation.4 | async-start | bytes 34603008 | tf_op jit(solution)/shard_map/all_gather | solution.py:55
  618.8 1.2 copy-start.10
Sparse Core Ops, SparseCore 0:
  181.2 372.3 all-gather.15
  555.6 139.6 all-gather.13
  697.4 38.7 all-gather.11
  738.2 380.5 all-gather.17
